TPU v7x, 32 devices: a whole 2x2x4 slice. The times are simulated.
32 devices in a mesh: grp: 2 (over y), tp: 8 (over z, x), sub: 2 (over core).
Axes of the slice: x: 2, y: 2, z: 4, core: 2. Of those that a mesh axis runs over, the one named last changes fastest.
Arguments:
- hidden_in: bfloat16 [32, 2, 4096], P('grp', 'sub', 'tp'), parts along dimension 0, may hold values from -16 to 16
- norm_attn: float32 [8192], replicated, may hold values from 0.25 to 1.75
- w_query: bfloat16 [8192, 2, 4096], P(None, 'sub', 'tp'), may hold values from -0.0625 to 0.0625
- w_key: bfloat16 [8192, 2, 512], P(None, 'sub', 'tp'), may hold values from -0.0625 to 0.0625
- w_value: bfloat16 [8192, 2, 512], P(None, 'sub', 'tp'), may hold values from -0.0625 to 0.0625
- w_out: bfloat16 [2, 4096, 2, 4096], P('sub', None, None, 'tp'), may hold values from -0.0625 to 0.0625
- norm_ffn: float32 [8192], replicated, may hold values from 0.25 to 1.75
- w_gate: bfloat16 [2, 4096, 14336], P('sub', None, 'tp'), may hold values from -0.0625 to 0.0625
- w_up: bfloat16 [2, 4096, 14336], P('sub', None, 'tp'), may hold values from -0.0625 to 0.0625
- w_down: bfloat16 [14336, 2, 4096], P('tp', 'sub'), may hold values from -0.0625 to 0.0625
- cache_keys: bfloat16 [32, 64, 8, 128], P('grp', 'tp', 'sub'), parts along dimension 0, may hold values from -250 to 250
- cache_values: bfloat16 [32, 64, 8, 128], P('grp', 'tp', 'sub'), parts along dimension 0, may hold values from -6 to 6
- lengths: int32 [32], P('grp'), parts along dimension 0, may hold values from 1 to 64, as said below
Outputs:
- hidden_out: bfloat16 [32, 2, 4096], P('grp', 'sub', 'tp'), parts along dimension 0
There are 2 independent parts, one for each index of `grp`. A program takes and returns all parts, laid end to end along the dimension named above; an argument that names none is the same for every part. Nothing has to cross between parts.
Inputs may be any that keep to these rules, and one draw needn't show every extreme that they name: `lengths`: some sequence has 64 live positions and some has 1.
All inputs are finite; a program needn't handle non-finite values.
Results may differ from a plain program's by a relative error of at most 0.012.
The roundings to bfloat16 on the way count: a program that leaves them out, or rounds other values in their place, can miss the bound.
Values may be sent and summed in bfloat16 or wider, within the bound.
A program may use at most 128 MiB of HBM per device.

v0:
```python
import math

import jax
import jax.numpy as jnp
from jax import lax
from jax.sharding import PartitionSpec as P

HD = 128


epsilon = 1e-05
rope_base = 500000.0
floor_score = -1e30


def joined(part, axis, combine):
    gathered = jax.tree.map(lambda a: lax.all_gather(a, axis), part)

    def take(source):
        return jax.tree.map(lambda a: lax.dynamic_index_in_dim(a, source, 0, False), gathered)

    return lax.fori_loop(
        1, lax.axis_size(axis), lambda source, state: combine(state, take(source)), take(0)
    )


def rope_angles(lengths):
    frequencies = rope_base ** (-(jnp.arange(HD // 2, dtype=jnp.float32) * 2.0) / HD)
    return lengths.astype(jnp.float32)[:, None] * frequencies[None, :]


def rotate(vectors, angles):
    middle_index = vectors.shape[-1] // 2
    cosine = jnp.cos(angles)[:, None, :]
    sine = jnp.sin(angles)[:, None, :]
    lower = vectors[..., :middle_index]
    upper = vectors[..., middle_index:]
    return jnp.concatenate([lower * cosine - upper * sine, upper * cosine + lower * sine], axis=-1)


def spread_rows(shard):
    across = lax.all_gather(shard, "tp", axis=2, tiled=True)
    return lax.all_gather(across, "sub", axis=1, tiled=True)


def half_rows_of(shard):
    return lax.all_gather(shard, "tp", axis=2, tiled=True)


def join_partials(earlier, later):
    earlier_max, earlier_sum, earlier_out = earlier
    later_max, later_sum, later_out = later
    highest = jnp.maximum(earlier_max, later_max)
    earlier_scale = jnp.exp(earlier_max - highest)
    later_scale = jnp.exp(later_max - highest)
    joined_sum = earlier_sum * earlier_scale + later_sum * later_scale
    joined_out = earlier_out * earlier_scale[..., None] + later_out * later_scale[..., None]
    return (highest, joined_sum, joined_out)


def per_device(
    hidden_in,
    norm_attn,
    w_query,
    w_key,
    w_value,
    w_out,
    norm_ffn,
    w_gate,
    w_up,
    w_down,
    cache_keys,
    cache_values,
    lengths,
):
    seq_count = hidden_in.shape[0]
    shard_width = hidden_in.shape[2]
    half_width = shard_width * lax.axis_size("tp")
    model_width = half_width * lax.axis_size("sub")
    tp_pos = lax.axis_index("tp")
    sub_pos = lax.axis_index("sub")
    residual = hidden_in.astype(jnp.float32)
    whole_rows = spread_rows(hidden_in).astype(jnp.float32)
    factor = lax.rsqrt(jnp.mean(whole_rows * whole_rows, axis=(1, 2)) + epsilon)
    gain_whole = norm_attn.reshape(whole_rows.shape[1], half_width)
    gathered = (whole_rows * factor[:, None, None] * gain_whole).astype(jnp.bfloat16)
    flattened = gathered.reshape(seq_count, model_width)
    query_part = jnp.dot(
        flattened, w_query.reshape(model_width, -1), preferred_element_type=jnp.float32
    ).astype(jnp.bfloat16)
    key_part = jnp.dot(
        flattened, w_key.reshape(model_width, -1), preferred_element_type=jnp.float32
    ).astype(jnp.bfloat16)
    value_part = jnp.dot(
        flattened, w_value.reshape(model_width, -1), preferred_element_type=jnp.float32
    ).astype(jnp.bfloat16)
    query, key_new, value_new = (
        lax.all_gather(query_part, "tp", axis=1, tiled=True),
        lax.all_gather(key_part, "tp", axis=1, tiled=True),
        lax.all_gather(value_part, "tp", axis=1, tiled=True),
    )
    query_heads = query.shape[1] // HD
    kv_heads = key_new.shape[1] // HD
    group_size = query_heads // kv_heads
    angles = rope_angles(lengths)
    query_rot = rotate(
        query.astype(jnp.float32).reshape(seq_count, query_heads, HD), angles
    ).astype(jnp.bfloat16)
    key_rot = rotate(key_new.astype(jnp.float32).reshape(seq_count, kv_heads, HD), angles).astype(
        jnp.bfloat16
    )
    grouped = query_rot.reshape(seq_count, kv_heads, group_size, HD)
    values_new = value_new.astype(jnp.float32).reshape(seq_count, kv_heads, 1, HD)
    span = cache_keys.shape[1]
    scores = jnp.einsum(
        "bkgd,blkd->bkgl", grouped, cache_keys, preferred_element_type=jnp.float32
    ) / math.sqrt(HD)
    places = tp_pos * span + jnp.arange(span, dtype=jnp.int32)
    live = (places[None, :] < lengths[:, None])[:, None, None, :]
    masked = jnp.where(live, scores, floor_score)
    local_max = jnp.max(masked, axis=-1)
    weights = jnp.where(live, jnp.exp(masked - local_max[..., None]), 0.0)
    local_sum = jnp.sum(weights, axis=-1)
    local_out = jnp.einsum(
        "bkgl,blkd->bkgd",
        weights,
        cache_values.astype(jnp.float32),
        precision=lax.Precision.HIGHEST,
    )
    own_score = jnp.sum(
        grouped.astype(jnp.float32) * key_rot.astype(jnp.float32)[:, :, None, :], axis=-1
    ) / math.sqrt(HD)
    joined_max, joined_sum, joined_out = joined(
        (local_max, local_sum, local_out), "tp", join_partials
    )
    highest = jnp.maximum(joined_max, own_score)
    kept_scale = jnp.exp(joined_max - highest)
    own_weight = jnp.exp(own_score - highest)
    numerator = joined_out * kept_scale[..., None] + own_weight[..., None] * values_new
    denominator = joined_sum * kept_scale + own_weight
    attended = (numerator / denominator[..., None]).reshape(seq_count, -1).astype(jnp.bfloat16)
    out_part = jnp.dot(
        attended, w_out.reshape(attended.shape[1], -1), preferred_element_type=jnp.float32
    )
    out_part = out_part.reshape(seq_count, -1, shard_width)
    mixed = lax.psum_scatter(out_part, "sub", scatter_dimension=1, tiled=True)
    middle = (residual + mixed).astype(jnp.bfloat16)
    middle_float = middle.astype(jnp.float32)
    raw_half = half_rows_of(middle).astype(jnp.float32)
    partial_squares = jnp.sum(raw_half * raw_half, axis=(1, 2))
    squares_mid = lax.psum(partial_squares, "sub")
    factor_mid = lax.rsqrt(squares_mid / model_width + epsilon)
    gain_half = lax.dynamic_slice_in_dim(norm_ffn, sub_pos * half_width, half_width)
    half_rows = (raw_half * factor_mid[:, None, None] * gain_half).astype(jnp.bfloat16)
    half_flat = half_rows.reshape(seq_count, half_width)
    gate_part = jnp.dot(
        half_flat, w_gate.reshape(half_width, -1), preferred_element_type=jnp.float32
    )
    up_part = jnp.dot(half_flat, w_up.reshape(half_width, -1), preferred_element_type=jnp.float32)
    gate_total, up_total = lax.psum((gate_part, up_part), "sub")
    hidden = (jax.nn.silu(gate_total) * up_total).astype(jnp.bfloat16)
    down_part = jnp.dot(
        hidden, w_down.reshape(hidden.shape[1], -1), preferred_element_type=jnp.float32
    )
    down_total = lax.psum(down_part, "tp")
    down_share = lax.dynamic_slice_in_dim(down_total, tp_pos * shard_width, shard_width, 1)
    return (middle_float + down_share[:, None, :]).astype(jnp.bfloat16)


def solution(mesh):
    in_specs = (
        P("grp", "sub", "tp"),
        P(),
        P(None, "sub", "tp"),
        P(None, "sub", "tp"),
        P(None, "sub", "tp"),
        P("sub", None, None, "tp"),
        P(),
        P("sub", None, "tp"),
        P("sub", None, "tp"),
        P("tp", "sub", None),
        P("grp", "tp", "sub", None),
        P("grp", "tp", "sub", None),
        P("grp"),
    )
    out_specs = P("grp", "sub", "tp")
    return jax.shard_map(
        per_device, mesh=mesh, in_specs=in_specs, out_specs=out_specs, check_vma=False
    )
```

profile of v0, /device:TPU:0, one launch (start us, length us, event | category | flops | bytes accessed | tf_op | source)
XLA Modules:
  0.0 410.7 jit_solution(6426538400944346462)
XLA Ops:
  6.6 32.7 %all_gather.36 = bf16[16,1,4096]{2,0,1:T(8,128)(2,1)S(1)} all-gather(bf16[16,1,512]{2,0,1:T(8,128)(2,1)} %param.15), channel_id=1, replica_groups=mesh['grp'=2,'tp'=8,'sub'=2] {'tp'}, dimensions={2}, use_global_device_ids=true | all-gather | bytes 147456 | tf_op jit(solution)/shard_map/all_gather | solution.py:42
  39.3 2.0 all_gather.37
  41.3 0.2 fusion.19
  41.5 0.8 mul.255
  42.3 0.1 fusion.25
  42.4 4.6 %fusion.12 = bf16[16,512]{1,0:T(8,128)(2,1)S(1)} fusion(bf16[16,8192]{1,0:T(8,128)(2,1)S(1)} %bitcast.90, bf16[8192,1,512]{2,0,1:T(8,128)(2,1)} %param.17), kind=kOutput, calls=%fused_computation.18 | convolution fusion | flops 134225920 | bytes 8667136 | tf_op jit(solution)/shard_map/dot_general | solution.py:88
  47.0 30.5 %all_gather.38 = bf16[16,4096]{1,0:T(8,128)(2,1)S(1)} all-gather(bf16[16,512]{1,0:T(8,128)(2,1)S(1)} %fusion.12), channel_id=1, replica_groups=mesh['grp'=2,'tp'=8,'sub'=2] {'tp'}, dimensions={1}, use_global_device_ids=true | all-gather | bytes 147456 | tf_op jit(solution)/shard_map/all_gather | solution.py:98
  77.7 0.1 multiply_cosine_fusion
  77.8 0.1 fusion.28
  78.0 0.3 fusion.48
  78.3 1.3 fusion.26
  79.7 0.2 fusion.27
  79.9 31.0 %all-gather.1 = f32[128,4,8]{2,1,0:T(4,128)S(1)} all-gather(f32[16,4,8]{2,1,0:T(4,128)S(1)} %fusion.27), channel_id=3, replica_groups=mesh['grp'=2,'tp'=8,'sub'=2] {'tp'}, dimensions={0}, use_global_device_ids=true | all-gather | bytes 18432 | tf_op jit(solution)/shard_map/all_gather | solution.py:17
  110.9 0.1 copy.68
  111.0 0.1 copy.66
  111.1 31.7 %all-gather = f32[128,4,8]{2,1,0:T(4,128)S(1)} all-gather(f32[16,4,8]{2,1,0:T(4,128)S(1)} %get-tuple-element.236), channel_id=2, replica_groups=mesh['grp'=2,'tp'=8,'sub'=2] {'tp'}, dimensions={0}, use_global_device_ids=true | all-gather | bytes 18432 | tf_op jit(solution)/shard_map/all_gather | solution.py:17
  142.8 0.1 copy.67
  142.9 0.1 copy.65
  143.0 0.4 fusion.15
  143.4 30.6 %all-gather.3 = bf16[8,64,16]{1,2,0:T(8,128)(2,1)S(1)} all-gather(bf16[1,64,16]{1,2,0:T(8,128)(2,1)S(1)} %fusion.15), channel_id=1, replica_groups=mesh['grp'=2,'tp'=8,'sub'=2] {'tp'}, dimensions={0}, use_global_device_ids=true | all-gather | bytes 18432 | tf_op jit(solution)/shard_map/all_gather | solution.py:99
  174.2 0.1 subtract_convert_fusion.1
  174.2 0.1 maximum_convert_fusion
  174.3 0.3 multiply_reduce_fusion
  174.6 0.1 copy.70
  174.7 0.4 fusion.16
  175.1 30.6 %all-gather.4 = bf16[8,64,16]{1,2,0:T(8,128)(2,1)S(1)} all-gather(bf16[1,64,16]{1,2,0:T(8,128)(2,1)S(1)} %fusion.16), channel_id=1, replica_groups=mesh['grp'=2,'tp'=8,'sub'=2] {'tp'}, dimensions={0}, use_global_device_ids=true | all-gather | bytes 18432 | tf_op jit(solution)/shard_map/all_gather | solution.py:100
  205.8 9.3 %copy.83 = bf16[512,8,2,512]{3,1,2,0:T(8,128)(2,1)} copy(bf16[512,8,2,512]{3,2,1,0:T(2,128)(2,1)} %bitcast.89) | data formatting | bytes 16777216
  215.1 11.4 %copy.75 = bf16[1024,4096]{1,0:T(8,128)(2,1)} copy(bf16[1024,4096]{0,1:T(8,128)(2,1)} %bitcast.88) | data formatting | bytes 16777216 | tf_op jit(solution)/shard_map/dot_general | solution.py:142
  226.5 1.0 slice.26
  227.5 10.0 %while.19 = (s32[]{:T(128)}, f32[16,4,8]{0,2,1:T(8,128)S(1)}, f32[16,4,8]{0,2,1:T(8,128)S(1)}, f32[16,4,8,128]{3,2,1,0:T(8,128)S(1)}, f32[8,16,4,8]{1,3,2,0:T(8,...) while((s32[]{:T(128)}, f32[16,4,8]{0,2,1:T(8,128)S(1)}, ...), condition=%wide.region_4.5_spmd, body=%wide.region_3.4_spmd.sunk | while | flops 199685 | bytes 815255 | solution.py:22
  227.5 0.1 copy.92
  227.7 1.2 fusion.58
  228.9 0.1 copy.92
  229.0 0.1 copy.93
  229.1 1.2 fusion.58
  230.4 0.1 copy.92
  230.4 0.1 copy.93
  230.5 1.2 fusion.58
  231.8 0.1 copy.92
  231.9 0.1 copy.93
  231.9 1.2 fusion.58
  233.2 0.1 copy.92
  233.4 1.2 fusion.58
  234.6 0.1 copy.92
  234.7 0.1 copy.93
  234.8 1.2 fusion.58
  236.1 0.1 copy.92
  236.1 0.1 copy.93
  236.2 1.2 fusion.58
  237.5 0.1 copy.71
  237.6 0.1 copy.72
  237.7 0.3 divide_convert_fusion
  238.1 6.3 %fusion.49 = f32[16,2,512]{2,0,1:T(8,128)} fusion(bf16[16,4096,1]{1,0,2:T(8,128)(2,1)S(1)} %reshape.198, bf16[2,512,4096]{2,1,0:T(8,128)(2,1)} %bitcast.87), kind=kOutput, calls=%fused_computation.77 | convolution fusion | flops 134217728 | bytes 8585216 | tf_op jit(solution)/shard_map/dot_general | solution.py:142
  244.5 8.5 %reduce-scatter.2.cloned.1.call-done = f32[16,1,512]{2,0,1:T(8,128)} async-done(((f32[16,2,512]{2,0,1:T(8,128)}), f32[16,1,512]{2,0,1:T(8,128)}) %reduce-scatter.2.cloned.1.call-update) | async-done | bytes 32784 | tf_op jit(solution)/shard_map/reduce_scatter | solution.py:146
  253.0 0.8 add_convert_fusion.1
  253.8 30.8 %all_gather.47 = bf16[16,1,4096]{2,0,1:T(8,128)(2,1)S(1)} all-gather(bf16[16,1,512]{2,0,1:T(8,128)(2,1)S(1)} %add_convert_fusion.1), channel_id=1, replica_groups=mesh['grp'=2,'tp'=8,'sub'=2] {'tp'}, dimensions={2}, use_global_device_ids=true | all-gather | bytes 147456 | tf_op jit(solution)/shard_map/all_gather | solution.py:47
  284.5 0.1 fusion.22
  284.7 2.6 psum.28
  287.3 7.9 %fusion.7 = f32[16,1792]{1,0:T(8,128)} fusion(bf16[1,4096,1792]{2,1,0:T(8,128)(2,1)} %param.22, bf16[16,1,4096]{2,0,1:T(8,128)(2,1)S(1)} %all_gather.47, f32[4096]{0:T(1024)S(1)} %dynamic_slice.50, f32[16]{0:T(128)S(1)} %add_rsqrt_fusion), kind=kOutput, calls=%fused_computation.12 | convolution fusion | flops 235143168 | bytes 14942272 | tf_op jit(solution)/shard_map/dot_general | solution.py:156
  295.2 7.9 %fusion.5 = f32[16,1792]{1,0:T(8,128)} fusion(bf16[1,4096,1792]{2,1,0:T(8,128)(2,1)} %param.23, bf16[16,1,4096]{2,0,1:T(8,128)(2,1)S(1)} %all_gather.47, f32[4096]{0:T(1024)S(1)} %dynamic_slice.50, f32[16]{0:T(128)S(1)} %add_rsqrt_fusion), kind=kOutput, calls=%fused_computation.10 | convolution fusion | flops 235143168 | bytes 14942272 | tf_op jit(solution)/shard_map/dot_general | solution.py:159
  303.2 19.1 %all-reduce.6.cloned.1.call-done = (f32[16,1792]{1,0:T(8,128)}, f32[16,1792]{1,0:T(8,128)}) async-done(((f32[16,1792]{1,0:T(8,128)}, f32[16,1792]{1,0:T(8,128)}), (f32[16,1792]{1,0:T(8,128)}, f32[16,1792]{1,0:T(8,128)})) %all-reduce.6.cloned.1.call-update) | async-done | bytes 229392 | tf_op jit(solution)/shard_map/psum | solution.py:160
  322.4 8.0 %fusion.3 = f32[16,4096]{1,0:T(8,128)} fusion(bf16[1792,1,4096]{2,0,1:T(8,128)(2,1)} %param.24, f32[16,1792]{1,0:T(8,128)} %get-tuple-element.221, f32[16,1792]{1,0:T(8,128)} %get-tuple-element.222), kind=kOutput, calls=%fused_computation.8 | convolution fusion | flops 235053056 | bytes 15171584 | tf_op jit(solution)/shard_map/dot_general | solution.py:162
  330.4 72.4 %all-reduce.4.cloned.1.call-done = f32[16,4096]{1,0:T(8,128)} async-done(((f32[16,4096]{1,0:T(8,128)}), f32[16,4096]{1,0:T(8,128)}) %all-reduce.4.cloned.1.call-update) | async-done | bytes 262160 | tf_op jit(solution)/shard_map/psum | solution.py:165
  402.8 1.4 fusion.37
  (55 shorter events, 1.2 us)
Async XLA Ops:
  6.5 136.5 %copy-start = (bf16[8192,1,64]{0,2,1:T(8,128)(2,1)S(1)}, bf16[8192,1,64]{0,2,1:T(8,128)(2,1)}, u32[]{:S(2)}) copy-start(bf16[8192,1,64]{0,2,1:T(8,128)(2,1)} %param.18) | copy-start | bytes 3145732
  6.5 71.1 %copy-start.7 = (s32[16]{0:T(128)S(1)}, s32[16]{0:T(128)}, u32[]{:S(2)}) copy-start(s32[16]{0:T(128)} %param.27) | copy-start | bytes 196
  6.5 71.4 %copy-start.3 = (bf16[16,8,4,128]{3,2,1,0:T(4,128)(2,1)S(1)}, bf16[16,8,4,128]{3,2,1,0:T(4,128)(2,1)}, u32[]{:S(2)}) copy-start(bf16[16,8,4,128]{3,2,1,0:T(4,128)(2,1)} %param.25) | copy-start | bytes 393220
  6.5 71.8 %copy-start.4 = (bf16[16,8,4,128]{3,2,1,0:T(4,128)(2,1)S(1)}, bf16[16,8,4,128]{3,2,1,0:T(4,128)(2,1)}, u32[]{:S(2)}) copy-start(bf16[16,8,4,128]{3,2,1,0:T(4,128)(2,1)} %param.26) | copy-start | bytes 393220
  6.5 168.1 %copy-start.2 = (bf16[8192,1,64]{0,2,1:T(8,128)(2,1)S(1)}, bf16[8192,1,64]{0,2,1:T(8,128)(2,1)}, u32[]{:S(2)}) copy-start(bf16[8192,1,64]{0,2,1:T(8,128)(2,1)} %param.19) | copy-start | bytes 3145732
  6.5 219.9 %all-gather.7.cloned.1.call-start = ((), (), s32[]{:S(2)}) async-start(), calls=%async_computation.3 | async-start | bytes 2359296 | tf_op jit(solution)/shard_map/all_gather | solution.py:17
  79.7 173.3 %reduce-scatter.2.cloned.1.call-start = ((), (), s32[]{:S(2)}) async-start(), calls=%async_computation.1 | async-start | bytes 98304 | tf_op jit(solution)/shard_map/reduce_scatter | solution.py:146
  215.1 29.3 %copy-start.6 = (f32[8192]{0:T(1024)S(1)}, f32[8192]{0:T(1024)}, u32[]{:S(2)}) copy-start(f32[8192]{0:T(1024)} %param.21) | copy-start | bytes 98308
  215.1 37.9 %copy-start.5 = (bf16[16,1,512]{2,0,1:T(8,128)(2,1)S(1)}, bf16[16,1,512]{2,0,1:T(8,128)(2,1)}, u32[]{:S(2)}) copy-start(bf16[16,1,512]{2,0,1:T(8,128)(2,1)} %param.15) | copy-start | bytes 49156
  244.4 78.0 %all-reduce.6.cloned.1.call-start = ((), (), s32[]{:S(2)}) async-start(), calls=%async_computation.4 | async-start | bytes 458752 | tf_op jit(solution)/shard_map/psum | solution.py:160
  295.2 109.0 %copy-start.1 = (bf16[8192,1,64]{0,2,1:T(8,128)(2,1)S(1)}, bf16[8192,1,64]{0,2,1:T(8,128)(2,1)}, u32[]{:S(2)}) copy-start(bf16[8192,1,64]{0,2,1:T(8,128)(2,1)} %param.18) | copy-start | bytes 3145732
  303.2 99.6 %all-reduce.4.cloned.1.call-start = ((), (), s32[]{:S(2)}) async-start(), calls=%async_computation.2 | async-start | bytes 524288 | tf_op jit(solution)/shard_map/psum | solution.py:165
Sparse Core Ops, SparseCore 0:
  79.8 53.2 all-gather.6
  244.5 8.4 reduce-scatter.1
  303.3 19.0 all-reduce.5
  330.5 72.2 all-reduce.3
where the time goes:
time: 412 us; the launch traced here: 411 us
  blocking collectives  223 us (54%)
  waiting for transfers between devices  100 us (24%)
  matrix products  37.1 us (9%)
  local copies, waits for them, and re-layouts  24.6 us (6%)
  between operations  13.3 us (3%)
  other arithmetic  12.6 us (3%)
    psum x1, waiting for transfers between devices, per_device(): down_total = lax.psum(down_part, 'tp')  72.4 us
    all_gather x2, blocking collectives, joined(): gathered = jax.tree.map(lambda a: lax.all_gather(a, axis), part)  62.7 us
    all_gather x1, blocking collectives, spread_rows(): across = lax.all_gather(shard, 'tp', axis=2, tiled=True)  32.7 us
    all_gather x1, blocking collectives, half_rows_of(): return lax.all_gather(shard, 'tp', axis=2, tiled=True)  30.8 us
    all_gather x1, blocking collectives, per_device(): lax.all_gather(key_part, 'tp', axis=1, tiled=True)  30.6 us
    all_gather x1, blocking collectives, per_device(): lax.all_gather(value_part, 'tp', axis=1, tiled=True)  30.6 us
    all_gather x1, blocking collectives, per_device(): lax.all_gather(query_part, 'tp', axis=1, tiled=True)  30.5 us
    psum x1, waiting for transfers between devices, per_device(): gate_total, up_total = lax.psum((gate_part, up_part), 'sub')  19.1 us
  transfers between devices with their start and end apart: 4, of which 3 were waited for; matrix products, arithmetic and copies ran while one was open for 6% of the time, Pallas kernels for 0%

commit v1 on v0

--- a/solution.py
+++ b/solution.py
@@ -1,8 +1,11 @@
+import functools
 import math
 
 import jax
 import jax.numpy as jnp
 from jax import lax
+from jax.experimental import pallas as pl
+from jax.experimental.pallas import tpu as pltpu
 from jax.sharding import PartitionSpec as P
 
 HD = 128
@@ -58,7 +61,7 @@
     return (highest, joined_sum, joined_out)
 
 
-def per_device(
+def per_device_plain(
     hidden_in,
     norm_attn,
     w_query,
@@ -167,6 +170,555 @@
     return (middle_float + down_share[:, None, :]).astype(jnp.bfloat16)
 
 
+MESH_ID = pl.DeviceIdType.MESH
+F32 = jnp.float32
+BF16 = jnp.bfloat16
+NT = (((1,), (1,)), ((), ()))
+
+
+def matmul(a, b):
+    return jnp.dot(a, b, preferred_element_type=F32)
+
+
+def remote(src, dst, send, recv, tp, sub):
+    return pltpu.make_async_remote_copy(
+        src_ref=src,
+        dst_ref=dst,
+        send_sem=send,
+        recv_sem=recv,
+        device_id={"tp": tp, "sub": sub},
+        device_id_type=MESH_ID,
+    )
+
+
+def step_kernel(
+    cfg,
+    x_ref,
+    aux_ref,
+    gain1_ref,
+    gain2_ref,
+    wq_hbm,
+    wk_hbm,
+    wv_hbm,
+    wo_hbm,
+    wg_hbm,
+    wu_hbm,
+    wd_hbm,
+    ck_hbm,
+    cv_hbm,
+    out_ref,
+    wq,
+    wk,
+    wv,
+    wo,
+    wg,
+    wu,
+    wd,
+    xg,
+    ckr,
+    cvr,
+    qkv,
+    qs,
+    qr,
+    ascr,
+    arow,
+    ab,
+    attf,
+    attb,
+    op,
+    orv,
+    mg,
+    nf,
+    gp,
+    gr,
+    hid,
+    dp,
+    dr,
+    w_sem,
+    c_sem,
+    xs_sem,
+    xr_sem,
+    cks_sem,
+    ckr_sem,
+    cvs_sem,
+    cvr_sem,
+    qs_sem,
+    qr_sem,
+    as_sem,
+    ar_sem,
+    o_sem,
+    ms_sem,
+    mr_sem,
+    gs_sem,
+    gr_sem,
+    ds_sem,
+    dr_sem,
+):
+    tp_n, sub_n, own, hpd, span, kvh = cfg
+    peers = tp_n * sub_n
+    seqs, width = x_ref.shape
+    model = peers * width
+    half = tp_n * width
+    t = lax.axis_index("tp")
+    s = lax.axis_index("sub")
+    me = s * tp_n + t
+
+    def load(i, src, dst):
+        return pltpu.make_async_copy(src, dst, w_sem.at[i])
+
+    loads = [
+        load(i, a, b)
+        for i, (a, b) in enumerate(
+            (
+                (wq_hbm, wq),
+                (wk_hbm, wk),
+                (wv_hbm, wv),
+                (wo_hbm, wo),
+                (wg_hbm, wg),
+                (wu_hbm, wu),
+                (wd_hbm, wd),
+            )
+        )
+    ]
+    for c in loads[:3]:
+        c.start()
+
+    barrier = pltpu.get_barrier_semaphore()
+
+    def greet(k, carry):
+        peer = lax.rem(me + k, peers)
+        pl.semaphore_signal(
+            barrier,
+            inc=1,
+            device_id={"tp": lax.rem(peer, tp_n), "sub": peer // tp_n},
+            device_id_type=MESH_ID,
+        )
+        return carry
+
+    lax.fori_loop(1, peers, greet, 0)
+    pl.semaphore_wait(barrier, peers - 1)
+
+    def spread(src, buf, ssem, rsem):
+        def one(k, carry):
+            peer = lax.rem(me + k, peers)
+            remote(
+                src, buf.at[me], ssem.at[k], rsem.at[me], lax.rem(peer, tp_n), peer // tp_n
+            ).start()
+            return carry
+
+        lax.fori_loop(1, peers, one, 0)
+
+    def spread_wait(buf, ssem, rsem):
+        def one(k, carry):
+            peer = lax.rem(me + k, peers)
+            remote(buf.at[peer], buf.at[peer], ssem.at[k], rsem.at[peer], t, s).wait_recv()
+            return carry
+
+        lax.fori_loop(1, peers, one, 0)
+
+    def spread_done(src, ssem, rsem):
+        def one(k, carry):
+            remote(src, src, ssem.at[k], rsem.at[me], t, s).wait_send()
+            return carry
+
+        lax.fori_loop(1, peers, one, 0)
+
+    def send_tp(src_of, buf, ssem, rsem):
+        def one(k, carry):
+            peer = lax.rem(t + k, tp_n)
+            remote(src_of(peer), buf.at[t], ssem.at[k], rsem.at[t], peer, s).start()
+            return carry
+
+        lax.fori_loop(1, tp_n, one, 0)
+
+    def wait_tp(buf, ssem, rsem):
+        def one(k, carry):
+            peer = lax.rem(t + k, tp_n)
+            remote(buf.at[peer], buf.at[peer], ssem.at[k], rsem.at[peer], t, s).wait_recv()
+            return carry
+
+        lax.fori_loop(1, tp_n, one, 0)
+
+    def done_tp(src_of, buf, ssem, rsem):
+        def one(k, carry):
+            peer = lax.rem(t + k, tp_n)
+            remote(src_of(peer), buf.at[t], ssem.at[k], rsem.at[t], peer, s).wait_send()
+            return carry
+
+        lax.fori_loop(1, tp_n, one, 0)
+
+    spread(x_ref, xg, xs_sem, xr_sem)
+    xg[me] = x_ref[...]
+
+    def ck_of(peer):
+        return ck_hbm.at[pl.ds(peer * own, own)]
+
+    def cv_of(peer):
+        return cv_hbm.at[pl.ds(peer * own, own)]
+
+    send_tp(ck_of, ckr, cks_sem, ckr_sem)
+    send_tp(cv_of, cvr, cvs_sem, cvr_sem)
+    own_k = pltpu.make_async_copy(ck_of(t), ckr.at[t], c_sem.at[0])
+    own_v = pltpu.make_async_copy(cv_of(t), cvr.at[t], c_sem.at[1])
+    own_k.start()
+    own_v.start()
+    loads[3].start()
+
+    spread_wait(xg, xs_sem, xr_sem)
+
+    def squares(c, acc):
+        v = xg[c].astype(F32)
+        return acc + jnp.sum(v * v, axis=1, keepdims=True)
+
+    total = lax.fori_loop(0, peers, squares, jnp.zeros((seqs, 1), F32))
+    factor = lax.rsqrt(total / model + epsilon)
+    for c in loads[:3]:
+        c.wait()
+    for c in loads[4:]:
+        c.start()
+
+    def project(c, carry):
+        q, k, v = carry
+        at = pl.ds(pl.multiple_of(c * width, width), width)
+        n = (xg[c].astype(F32) * factor * gain1_ref[:, at]).astype(BF16)
+        q = q + matmul(n, wq[at, :])
+        k = k + lax.dot_general(n, wk[:, at], NT, preferred_element_type=F32)
+        v = v + lax.dot_general(n, wv[:, at], NT, preferred_element_type=F32)
+        return q, k, v
+
+    kvw = wk.shape[0]
+    q, k, v = lax.fori_loop(
+        0,
+        peers,
+        project,
+        (
+            jnp.zeros((seqs, width), F32),
+            jnp.zeros((seqs, kvw), F32),
+            jnp.zeros((seqs, kvw), F32),
+        ),
+    )
+    parts = HD // kvw
+    lane = lax.broadcasted_iota(jnp.int32, (seqs, HD), 1)
+    mine = lane // kvw == lax.rem(t, parts)
+    qkv[:, :width] = q.astype(BF16).astype(F32)
+    for n, value in enumerate((k, v)):
+        whole = jnp.concatenate([value.astype(BF16).astype(F32)] * parts, axis=1)
+        qkv[:, width + n * HD : width + (n + 1) * HD] = jnp.where(mine, whole, 0.0)
+    for d in range(tp_n):
+        qs[d] = qkv[d * own : (d + 1) * own, :]
+    qr[t] = qs[t]
+    send_tp(lambda peer: qs.at[peer], qr, qs_sem, qr_sem)
+
+    wait_tp(ckr, cks_sem, ckr_sem)
+    wait_tp(cvr, cvs_sem, cvr_sem)
+    own_k.wait()
+    own_v.wait()
+    wait_tp(qr, qs_sem, qr_sem)
+
+    rows = hpd * tp_n
+    cols = tp_n * span * kvh
+    row = lax.broadcasted_iota(jnp.int32, (rows, cols), 0)
+    col = lax.broadcasted_iota(jnp.int32, (rows, cols), 1)
+    same_head = lax.rem(row, tp_n) // parts == lax.rem(col, kvh)
+    place = (col // kvh).astype(F32)
+    pair_row = lax.broadcasted_iota(jnp.int32, (tp_n, tp_n), 0)
+    pair_col = lax.broadcasted_iota(jnp.int32, (tp_n, tp_n), 1)
+    pairs = jnp.where(pair_row // parts == pair_col // parts, 1.0, 0.0).astype(F32)
+    root = math.sqrt(HD)
+
+    def rope(value, cosine, sine):
+        turned = pltpu.roll(value, HD // 2, 1)
+        return (value * cosine + turned * sine).astype(BF16)
+
+    for i in range(own):
+        table = aux_ref[t * own + i]
+        cosine, sine, length = table[0:1], table[1:2], table[2:3, 0:1]
+        queries = jnp.concatenate(
+            [qr[:, i, j * HD : (j + 1) * HD] for j in range(hpd)], axis=0
+        )
+        query_rot = rope(queries, cosine, sine)
+        exact = lax.Precision.HIGHEST
+        key_new = jnp.dot(
+            pairs, qr[:, i, width : width + HD], precision=exact, preferred_element_type=F32
+        )
+        value_new = jnp.dot(
+            pairs,
+            qr[:, i, width + HD : width + 2 * HD],
+            precision=exact,
+            preferred_element_type=F32,
+        )
+        key_rot = rope(key_new, cosine, sine).astype(F32)
+        keys = ckr[:, i].reshape(cols, HD)
+        values = cvr[:, i].reshape(cols, HD).astype(F32)
+        scores = lax.dot_general(query_rot, keys, NT, preferred_element_type=F32) / root
+        live = same_head & (place < length)
+        masked = jnp.where(live, scores, floor_score)
+        key_all = jnp.concatenate([key_rot] * hpd, axis=0)
+        value_all = jnp.concatenate([value_new] * hpd, axis=0)
+        own_score = jnp.sum(query_rot.astype(F32) * key_all, axis=1, keepdims=True) / root
+        highest = jnp.maximum(jnp.max(masked, axis=1, keepdims=True), own_score)
+        weights = jnp.where(live, jnp.exp(masked - highest), 0.0)
+        own_weight = jnp.exp(own_score - highest)
+        numerator = jnp.dot(weights, values, precision=exact, preferred_element_type=F32)
+        numerator = numerator + own_weight * value_all
+        denominator = jnp.sum(weights, axis=1, keepdims=True) + own_weight
+        ascr[...] = numerator / denominator
+        for j in range(hpd):
+            for d in range(tp_n):
+                r = j * tp_n + d
+                head = d * hpd + j
+                arow[i : i + 1, head * HD : (head + 1) * HD] = ascr[r : r + 1, :]
+    ab[t] = arow[...].astype(BF16)
+    send_tp(lambda peer: ab.at[t], ab, as_sem, ar_sem)
+    wait_tp(ab, as_sem, ar_sem)
+    for d in range(tp_n):
+        attf[d * own : (d + 1) * own, :] = ab[d].astype(F32)
+    attb[...] = attf[...].astype(BF16)
+
+    loads[3].wait()
+
+    def mix(c, acc):
+        at = pl.ds(pl.multiple_of(c * width, width), width)
+        return acc + matmul(attb[:, at], wo[at, :])
+
+    mixed = lax.fori_loop(0, tp_n, mix, jnp.zeros((seqs, sub_n * width), F32))
+    for c in range(sub_n):
+        op[c] = mixed[:, c * width : (c + 1) * width]
+    other = 1 - s
+    swap = remote(op.at[other], orv, o_sem.at[0], o_sem.at[1], t, other)
+    swap.start()
+    swap.wait_recv()
+    middle = (x_ref[...].astype(F32) + (op[s] + orv[...])).astype(BF16)
+    mg[me] = middle
+    spread(mg.at[me], mg, ms_sem, mr_sem)
+    spread_wait(mg, ms_sem, mr_sem)
+
+    def squares_mid(c, acc):
+        v = mg[c].astype(F32)
+        return acc + jnp.sum(v * v, axis=1, keepdims=True)
+
+    total_mid = lax.fori_loop(0, peers, squares_mid, jnp.zeros((seqs, 1), F32))
+    factor_mid = lax.rsqrt(total_mid / model + epsilon)
+
+    def scale(c, carry):
+        at = pl.ds(pl.multiple_of(c * width, width), width)
+        gain_at = pl.ds(pl.multiple_of(s * half + c * width, width), width)
+        raw = mg[s * tp_n + c].astype(F32)
+        nf[:, at] = (raw * factor_mid * gain2_ref[:, gain_at]).astype(BF16)
+        return carry
+
+    lax.fori_loop(0, tp_n, scale, 0)
+    loads[4].wait()
+    loads[5].wait()
+    chunks, _, _, chunk = gp.shape
+
+    def gate_copy(n):
+        return remote(gp.at[n], gr.at[n], gs_sem.at[n], gr_sem.at[n], t, other)
+
+    def gates(n, carry):
+        at = pl.ds(pl.multiple_of(n * chunk, chunk), chunk)
+        normed = nf[...]
+        gp[n, 0] = matmul(normed, wg[:, at])
+        gp[n, 1] = matmul(normed, wu[:, at])
+        gate_copy(n).start()
+        return carry
+
+    lax.fori_loop(0, chunks, gates, 0)
+
+    def joins(n, carry):
+        gate_copy(n).wait_recv()
+        at = pl.ds(pl.multiple_of(n * chunk, chunk), chunk)
+        gate = gp[n, 0] + gr[n, 0]
+        up = gp[n, 1] + gr[n, 1]
+        hid[:, at] = (gate / (1.0 + jnp.exp(-gate)) * up).astype(BF16)
+        return carry
+
+    lax.fori_loop(0, chunks, joins, 0)
+    loads[6].wait()
+
+    def down(peer):
+        at = pl.ds(pl.multiple_of(peer * width, width), width)
+        return matmul(hid[...], wd[:, at])
+
+    def share(k, carry):
+        peer = lax.rem(t + k, tp_n)
+        dp[peer] = down(peer)
+        remote(dp.at[peer], dr.at[t], ds_sem.at[k], dr_sem.at[t], peer, s).start()
+        return carry
+
+    lax.fori_loop(1, tp_n, share, 0)
+    result = down(t)
+
+    def gather(k, acc):
+        peer = lax.rem(t + k, tp_n)
+        remote(dr.at[peer], dr.at[peer], ds_sem.at[k], dr_sem.at[peer], t, s).wait_recv()
+        return acc + dr[peer]
+
+    result = lax.fori_loop(1, tp_n, gather, result)
+    out_ref[...] = (mg[me].astype(F32) + result).astype(BF16)
+
+    spread_done(x_ref, xs_sem, xr_sem)
+    done_tp(ck_of, ckr, cks_sem, ckr_sem)
+    done_tp(cv_of, cvr, cvs_sem, cvr_sem)
+    done_tp(lambda peer: qs.at[peer], qr, qs_sem, qr_sem)
+    done_tp(lambda peer: ab.at[t], ab, as_sem, ar_sem)
+    swap.wait_send()
+    spread_done(mg.at[me], ms_sem, mr_sem)
+
+    def gates_done(n, carry):
+        gate_copy(n).wait_send()
+        return carry
+
+    lax.fori_loop(0, chunks, gates_done, 0)
+    done_tp(lambda peer: dp.at[peer], dr, ds_sem, dr_sem)
+
+
+def per_device(
+    hidden_in,
+    norm_attn,
+    w_query,
+    w_key,
+    w_value,
+    w_out,
+    norm_ffn,
+    w_gate,
+    w_up,
+    w_down,
+    cache_keys,
+    cache_values,
+    lengths,
+):
+    tp_n = lax.axis_size("tp")
+    sub_n = lax.axis_size("sub")
+    seqs, _, width = hidden_in.shape
+    model = norm_attn.shape[0]
+    half = width * tp_n
+    kvw = w_key.shape[2]
+    span, kvh = cache_keys.shape[1:3]
+    ff = w_gate.shape[2]
+    hpd = max(width // HD, 1)
+    own = max(seqs // tp_n, 1)
+    fits = (
+        sub_n == 2
+        and width % HD == 0
+        and ff % HD == 0
+        and seqs % tp_n == 0
+        and HD % kvw == 0
+        and w_query.shape[2] == width
+        and hpd * (HD // kvw) * kvh == hpd * tp_n
+        and (span * kvh) % 16 == 0
+    )
+    if not fits:
+        return per_device_plain(
+            hidden_in,
+            norm_attn,
+            w_query,
+            w_key,
+            w_value,
+            w_out,
+            norm_ffn,
+            w_gate,
+            w_up,
+            w_down,
+            cache_keys,
+            cache_values,
+            lengths,
+        )
+    peers = tp_n * sub_n
+    angles = rope_angles(lengths)
+    cosine = jnp.cos(angles)
+    sine = jnp.sin(angles)
+    long = jnp.broadcast_to(lengths.astype(F32)[:, None], (seqs, HD))
+    aux = jnp.stack(
+        [
+            jnp.concatenate([cosine, cosine], axis=1),
+            jnp.concatenate([-sine, sine], axis=1),
+            long,
+        ],
+        axis=1,
+    )
+    aux = jnp.pad(aux, ((0, 0), (0, 5), (0, 0)))
+    chunk = 2 * HD if ff % (2 * HD) == 0 else HD
+    chunks = ff // chunk
+    dma = pltpu.SemaphoreType.DMA
+    vmem = pltpu.VMEM
+    weights = [
+        w_query.reshape(model, width),
+        w_key.reshape(model, kvw).T,
+        w_value.reshape(model, kvw).T,
+        w_out.reshape(half, sub_n * width),
+        w_gate.reshape(half, ff),
+        w_up.reshape(half, ff),
+        w_down.reshape(ff, half),
+    ]
+    caches = [
+        cache_keys.reshape(seqs, span * kvh, HD),
+        cache_values.reshape(seqs, span * kvh, HD),
+    ]
+    wide = width + 2 * HD
+    out = pl.pallas_call(
+        functools.partial(step_kernel, (tp_n, sub_n, own, hpd, span, kvh)),
+        out_shape=jax.ShapeDtypeStruct((seqs, width), BF16),
+        in_specs=[pl.BlockSpec(memory_space=pltpu.VMEM)] * 4
+        + [pl.BlockSpec(memory_space=pl.ANY)] * 9,
+        out_specs=pl.BlockSpec(memory_space=pltpu.VMEM),
+        scratch_shapes=[vmem(w.shape, BF16) for w in weights]
+        + [
+            vmem((peers, seqs, width), BF16),
+            vmem((tp_n, own, span * kvh, HD), BF16),
+            vmem((tp_n, own, span * kvh, HD), BF16),
+            vmem((seqs, wide), F32),
+            vmem((tp_n, own, wide), F32),
+            vmem((tp_n, own, wide), F32),
+            vmem((hpd * tp_n, HD), F32),
+            vmem((own, half), F32),
+            vmem((tp_n, own, half), BF16),
+            vmem((seqs, half), F32),
+            vmem((seqs, half), BF16),
+            vmem((sub_n, seqs, width), F32),
+            vmem((seqs, width), F32),
+            vmem((peers, seqs, width), BF16),
+            vmem((seqs, half), BF16),
+            vmem((chunks, 2, seqs, chunk), F32),
+            vmem((chunks, 2, seqs, chunk), F32),
+            vmem((seqs, ff), BF16),
+            vmem((tp_n, seqs, width), F32),
+            vmem((tp_n, seqs, width), F32),
+            dma((7,)),
+            dma((2,)),
+            dma((peers,)),
+            dma((peers,)),
+            dma((tp_n,)),
+            dma((tp_n,)),
+            dma((tp_n,)),
+            dma((tp_n,)),
+            dma((tp_n,)),
+            dma((tp_n,)),
+            dma((tp_n,)),
+            dma((tp_n,)),
+            dma((2,)),
+            dma((peers,)),
+            dma((peers,)),
+            dma((chunks,)),
+            dma((chunks,)),
+            dma((tp_n,)),
+            dma((tp_n,)),
+        ],
+        compiler_params=pltpu.CompilerParams(
+            collective_id=0, has_side_effects=True, vmem_limit_bytes=67043328
+        ),
+        name="decode_step",
+    )(
+        hidden_in.reshape(seqs, width),
+        aux,
+        norm_attn.reshape(1, model),
+        norm_ffn.reshape(1, model),
+        *weights,
+        *caches,
+    )
+    return out.reshape(seqs, 1, width)
+
+
 def solution(mesh):
     in_specs = (
         P("grp", "sub", "tp"),

time: 412 us -> 70.4 us (0.17)
  blocking collectives: 223 us -> 0 us
  waiting for transfers between devices: 100 us -> 0 us
  Pallas kernels: 0 us -> 57.9 us
  matrix products: 37.1 us -> 0 us
  local copies, waits for them, and re-layouts: 24.6 us -> 10.7 us
  between operations: 13.3 us -> 0.02 us
  other arithmetic: 12.6 us -> 1.54 us
    all_gather x8 -> x0, blocking collectives: 220 us -> none  [the longest x2 62.7 us: joined(): gathered = jax.tree.map(lambda a: lax.all_gather(a, axis), part)]
    psum x2 -> x0, waiting for transfers between devices: 91.5 us -> none  [the longest x1 72.4 us: per_device(): down_total = lax.psum(down_part, 'tp')]
    pallas_call x0 -> x1, Pallas kernels: none -> 57.9 us  [per_device(): pl.pallas_call(functools.partial(step_kernel, (tp_n, sub_n, own, hpd, spa...]
    dot_general x9 -> x0, matrix products: 37.1 us -> none  [the longest x1 8.01 us: per_device(): jnp.dot(hidden, w_down.reshape(hidden.shape[1], -1), preferred_element_ty...]
    dot_general x1 -> x0, local copies, waits for them, and re-layouts: 11.4 us -> none  [per_device(): jnp.dot(attended, w_out.reshape(attended.shape[1], -1), preferred_element...]
    add x16 -> x0, other arithmetic: 8.68 us -> none  [the longest x7 8.5 us: join_partials(): earlier_out * earlier_scale[..., None] + later_out * later_scale[..., None]]
    reduce_scatter x1 -> x0, waiting for transfers between devices: 8.54 us -> none  [per_device(): mixed = lax.psum_scatter(out_part, 'sub', scatter_dimension=1, tiled=True)]
    unnamed x18 -> x2, local copies, waits for them, and re-layouts: 9.4 us -> 10.6 us
  transfers between devices with their start and end apart: 4 -> 0, of which waited for: 3 -> 0; matrix products, arithmetic and copies ran while one was open for 6% -> 0% of each run, Pallas kernels for 0% -> 0%
where the time goes in v1:
time: 70.4 us; the launch traced here: 70.2 us
  Pallas kernels  57.9 us (82%)
  local copies, waits for them, and re-layouts  10.7 us (15%)
  other arithmetic  1.54 us (2%)
    pallas_call x1, Pallas kernels, per_device(): pl.pallas_call(functools.partial(step_kernel, (tp_n, sub_n, own, hpd, spa...  57.9 us
    unnamed x2, local copies, waits for them, and re-layouts  10.6 us

profile of v1, /device:TPU:0, one launch (start us, length us, event | category | flops | bytes accessed | tf_op | source)
XLA Modules:
  0.0 70.2 jit_solution(6297662661229916252)
XLA Ops:
  0.0 0.7 convert_element_type.6
  0.7 0.1 stack_broadcast_in_dim.2
  0.7 0.1 multiply_cosine_fusion
  0.9 0.1 pad_maximum_fusion
  1.0 0.7 select_maximum_fusion.aux_ref
  1.6 9.3 %copy.15 = bf16[512,8,2,512]{3,1,2,0:T(8,128)(2,1)} copy(bf16[512,8,2,512]{3,2,1,0:T(2,128)(2,1)} %bitcast.28) | data formatting | bytes 16777216
  10.9 57.9 %decode_step.1 = bf16[16,512]{1,0:T(8,128)(2,1)} custom-call(bf16[16,512]{1,0:T(8,128)(2,1)} %bitcast.38, f32[16,8,128]{2,1,0:T(8,128)} %select_maximum_fusion.aux_ref, f32[1,8192]{1,0:T(1,128)} %bitcast.34, f32[1,8192]{1,0:T(1,128)} %bitcast.35, bf16[8192,512]{1,0:T(8,128)(2,1)} %bitcast.27, bf16[64,8192]{1,0:T(8,128)(2,1)} %bitcast.29, ...), custom_call_target="tpu_custom_call" | custom-call | tf_op jit(solution)/shard_map/decode_step/pallas_call | solution.py:659
  68.8 1.3 %copy.17 = bf16[16,1,512]{2,0,1:T(8,128)(2,1)} copy(bf16[16,1,512]{2,0,1:T(8,128)(2,1)} %bitcast.33) | data formatting | bytes 32768
  (1 shorter events, 0.0 us)

commit v2 on v1

--- a/solution.py
+++ b/solution.py
@@ -253,6 +253,10 @@
     gr_sem,
     ds_sem,
     dr_sem,
+    xf_sem,
+    xh_sem,
+    mf_sem,
+    mh_sem,
 ):
     tp_n, sub_n, own, hpd, span, kvh = cfg
     peers = tp_n * sub_n
@@ -298,30 +302,48 @@
     lax.fori_loop(1, peers, greet, 0)
     pl.semaphore_wait(barrier, peers - 1)
 
-    def spread(src, buf, ssem, rsem):
+    other = 1 - s
+
+    def forward(src, buf, slot, peer, fsem, gsem):
+        return remote(src, buf.at[slot], fsem.at[peer], gsem.at[peer], t, other)
+
+    def spread(src, buf, ssem, rsem, fsem, gsem):
+        forward(src, buf, me, t, fsem, gsem).start()
+
         def one(k, carry):
-            peer = lax.rem(me + k, peers)
-            remote(
-                src, buf.at[me], ssem.at[k], rsem.at[me], lax.rem(peer, tp_n), peer // tp_n
-            ).start()
+            peer = lax.rem(t + k, tp_n)
+            remote(src, buf.at[me], ssem.at[k], rsem.at[t], peer, s).start()
             return carry
 
-        lax.fori_loop(1, peers, one, 0)
-
-    def spread_wait(buf, ssem, rsem):
+        lax.fori_loop(1, tp_n, one, 0)
+
+    def spread_wait(buf, ssem, rsem, fsem, gsem):
         def one(k, carry):
-            peer = lax.rem(me + k, peers)
-            remote(buf.at[peer], buf.at[peer], ssem.at[k], rsem.at[peer], t, s).wait_recv()
+            peer = lax.rem(t + k, tp_n)
+            slot = s * tp_n + peer
+            remote(buf.at[slot], buf.at[slot], ssem.at[k], rsem.at[peer], t, s).wait_recv()
+            forward(buf.at[slot], buf, slot, peer, fsem, gsem).start()
             return carry
 
-        lax.fori_loop(1, peers, one, 0)
-
-    def spread_done(src, ssem, rsem):
+        lax.fori_loop(1, tp_n, one, 0)
+
+        def two(peer, carry):
+            slot = other * tp_n + peer
+            forward(buf.at[slot], buf, slot, peer, fsem, gsem).wait_recv()
+            return carry
+
+        lax.fori_loop(0, tp_n, two, 0)
+
+    def spread_done(src, buf, ssem, rsem, fsem, gsem):
         def one(k, carry):
-            remote(src, src, ssem.at[k], rsem.at[me], t, s).wait_send()
+            peer = lax.rem(t + k, tp_n)
+            slot = s * tp_n + peer
+            remote(src, buf.at[me], ssem.at[k], rsem.at[t], peer, s).wait_send()
+            forward(buf.at[slot], buf, slot, peer, fsem, gsem).wait_send()
             return carry
 
-        lax.fori_loop(1, peers, one, 0)
+        lax.fori_loop(1, tp_n, one, 0)
+        forward(src, buf, me, t, fsem, gsem).wait_send()
 
     def send_tp(src_of, buf, ssem, rsem):
         def one(k, carry):
@@ -347,7 +369,7 @@
 
         lax.fori_loop(1, tp_n, one, 0)
 
-    spread(x_ref, xg, xs_sem, xr_sem)
+    spread(x_ref, xg, xs_sem, xr_sem, xf_sem, xh_sem)
     xg[me] = x_ref[...]
 
     def ck_of(peer):
@@ -362,9 +384,10 @@
     own_v = pltpu.make_async_copy(cv_of(t), cvr.at[t], c_sem.at[1])
     own_k.start()
     own_v.start()
-    loads[3].start()
-
-    spread_wait(xg, xs_sem, xr_sem)
+    for c in loads[3:]:
+        c.start()
+
+    spread_wait(xg, xs_sem, xr_sem, xf_sem, xh_sem)
 
     def squares(c, acc):
         v = xg[c].astype(F32)
@@ -374,13 +397,12 @@
     factor = lax.rsqrt(total / model + epsilon)
     for c in loads[:3]:
         c.wait()
-    for c in loads[4:]:
-        c.start()
 
     def project(c, carry):
         q, k, v = carry
-        at = pl.ds(pl.multiple_of(c * width, width), width)
-        n = (xg[c].astype(F32) * factor * gain1_ref[:, at]).astype(BF16)
+        at = pl.ds(pl.multiple_of(c * (4 * width), 4 * width), 4 * width)
+        raw = jnp.concatenate([xg[c * 4 + i] for i in range(4)], axis=1).astype(F32)
+        n = (raw * factor * gain1_ref[:, at]).astype(BF16)
         q = q + matmul(n, wq[at, :])
         k = k + lax.dot_general(n, wk[:, at], NT, preferred_element_type=F32)
         v = v + lax.dot_general(n, wv[:, at], NT, preferred_element_type=F32)
@@ -389,7 +411,7 @@
     kvw = wk.shape[0]
     q, k, v = lax.fori_loop(
         0,
-        peers,
+        peers // 4,
         project,
         (
             jnp.zeros((seqs, width), F32),
@@ -408,6 +430,18 @@
         qs[d] = qkv[d * own : (d + 1) * own, :]
     qr[t] = qs[t]
     send_tp(lambda peer: qs.at[peer], qr, qs_sem, qr_sem)
+
+    loads[3].wait()
+    strip = 2 * HD
+
+    def relay(n, carry):
+        base = pl.multiple_of(n * strip, strip)
+        flat = wo[pl.ds(base, strip)].reshape(strip, sub_n * width)
+        for c in range(sub_n):
+            wq[pl.ds(base + c * half, strip), :] = flat[:, c * width : (c + 1) * width]
+        return carry
+
+    lax.fori_loop(0, half // strip, relay, 0)
 
     wait_tp(ckr, cks_sem, ckr_sem)
     wait_tp(cvr, cvs_sem, cvr_sem)
@@ -475,23 +509,20 @@
         attf[d * own : (d + 1) * own, :] = ab[d].astype(F32)
     attb[...] = attf[...].astype(BF16)
 
-    loads[3].wait()
-
-    def mix(c, acc):
-        at = pl.ds(pl.multiple_of(c * width, width), width)
-        return acc + matmul(attb[:, at], wo[at, :])
-
-    mixed = lax.fori_loop(0, tp_n, mix, jnp.zeros((seqs, sub_n * width), F32))
-    for c in range(sub_n):
-        op[c] = mixed[:, c * width : (c + 1) * width]
-    other = 1 - s
+    attended = attb[...]
+
+    def mix(c, carry):
+        op[c] = matmul(attended, wq[pl.ds(pl.multiple_of(c * half, half), half), :])
+        return carry
+
+    lax.fori_loop(0, sub_n, mix, 0)
     swap = remote(op.at[other], orv, o_sem.at[0], o_sem.at[1], t, other)
     swap.start()
     swap.wait_recv()
     middle = (x_ref[...].astype(F32) + (op[s] + orv[...])).astype(BF16)
     mg[me] = middle
-    spread(mg.at[me], mg, ms_sem, mr_sem)
-    spread_wait(mg, ms_sem, mr_sem)
+    spread(mg.at[me], mg, ms_sem, mr_sem, mf_sem, mh_sem)
+    spread_wait(mg, ms_sem, mr_sem, mf_sem, mh_sem)
 
     def squares_mid(c, acc):
         v = mg[c].astype(F32)
@@ -542,7 +573,7 @@
 
     def share(k, carry):
         peer = lax.rem(t + k, tp_n)
-        dp[peer] = down(peer)
+        dp[peer] = down(peer).astype(BF16)
         remote(dp.at[peer], dr.at[t], ds_sem.at[k], dr_sem.at[t], peer, s).start()
         return carry
 
@@ -552,18 +583,18 @@
     def gather(k, acc):
         peer = lax.rem(t + k, tp_n)
         remote(dr.at[peer], dr.at[peer], ds_sem.at[k], dr_sem.at[peer], t, s).wait_recv()
-        return acc + dr[peer]
+        return acc + dr[peer].astype(F32)
 
     result = lax.fori_loop(1, tp_n, gather, result)
     out_ref[...] = (mg[me].astype(F32) + result).astype(BF16)
 
-    spread_done(x_ref, xs_sem, xr_sem)
+    spread_done(x_ref, xg, xs_sem, xr_sem, xf_sem, xh_sem)
     done_tp(ck_of, ckr, cks_sem, ckr_sem)
     done_tp(cv_of, cvr, cvs_sem, cvr_sem)
     done_tp(lambda peer: qs.at[peer], qr, qs_sem, qr_sem)
     done_tp(lambda peer: ab.at[t], ab, as_sem, ar_sem)
     swap.wait_send()
-    spread_done(mg.at[me], ms_sem, mr_sem)
+    spread_done(mg.at[me], mg, ms_sem, mr_sem, mf_sem, mh_sem)
 
     def gates_done(n, carry):
         gate_copy(n).wait_send()
@@ -600,6 +631,7 @@
     own = max(seqs // tp_n, 1)
     fits = (
         sub_n == 2
+        and tp_n % 2 == 0
         and width % HD == 0
         and ff % HD == 0
         and seqs % tp_n == 0
@@ -638,7 +670,7 @@
         axis=1,
     )
     aux = jnp.pad(aux, ((0, 0), (0, 5), (0, 0)))
-    chunk = 2 * HD if ff % (2 * HD) == 0 else HD
+    chunk = ff // 2 if ff % (2 * HD) == 0 else ff
     chunks = ff // chunk
     dma = pltpu.SemaphoreType.DMA
     vmem = pltpu.VMEM
@@ -646,7 +678,7 @@
         w_query.reshape(model, width),
         w_key.reshape(model, kvw).T,
         w_value.reshape(model, kvw).T,
-        w_out.reshape(half, sub_n * width),
+        w_out.reshape(half, sub_n, width),
         w_gate.reshape(half, ff),
         w_up.reshape(half, ff),
         w_down.reshape(ff, half),
@@ -682,12 +714,12 @@
             vmem((chunks, 2, seqs, chunk), F32),
             vmem((chunks, 2, seqs, chunk), F32),
             vmem((seqs, ff), BF16),
-            vmem((tp_n, seqs, width), F32),
-            vmem((tp_n, seqs, width), F32),
+            vmem((tp_n, seqs, width), BF16),
+            vmem((tp_n, seqs, width), BF16),
             dma((7,)),
             dma((2,)),
-            dma((peers,)),
-            dma((peers,)),
+            dma((tp_n,)),
+            dma((tp_n,)),
             dma((tp_n,)),
             dma((tp_n,)),
             dma((tp_n,)),
@@ -697,10 +729,14 @@
             dma((tp_n,)),
             dma((tp_n,)),
             dma((2,)),
-            dma((peers,)),
-            dma((peers,)),
+            dma((tp_n,)),
+            dma((tp_n,)),
             dma((chunks,)),
             dma((chunks,)),
+            dma((tp_n,)),
+            dma((tp_n,)),
+            dma((tp_n,)),
+            dma((tp_n,)),
             dma((tp_n,)),
             dma((tp_n,)),
         ],

time: 70.4 us -> 53 us (0.75)
  local copies, waits for them, and re-layouts: 10.7 us -> 1.4 us
  Pallas kernels: 57.9 us -> 49.8 us
    unnamed x2 -> x1, local copies, waits for them, and re-layouts: 10.6 us -> 1.32 us
    pallas_call x1, Pallas kernels: 57.9 us -> 49.8 us  [per_device(): pl.pallas_call(functools.partial(step_kernel, (tp_n, sub_n, own, hpd, spa...]
where the time goes in v2:
time: 53 us; the launch traced here: 52.7 us
  Pallas kernels  49.8 us (94%)
  other arithmetic  1.52 us (3%)
  local copies, waits for them, and re-layouts  1.4 us (3%)
    pallas_call x1, Pallas kernels, per_device(): pl.pallas_call(functools.partial(step_kernel, (tp_n, sub_n, own, hpd, spa...  49.8 us
    unnamed x1, local copies, waits for them, and re-layouts  1.32 us

profile of v2, /device:TPU:0, one launch (start us, length us, event | category | flops | bytes accessed | tf_op | source)
XLA Modules:
  0.0 52.7 jit_solution(6079289849496357828)
XLA Ops:
  0.0 0.7 %convert_element_type.6 = f32[16]{0:T(128)S(1)} convert(s32[16]{0:T(128)} %param.25) | non-fusion elementwise | flops 16 | bytes 128 | tf_op jit(solution)/shard_map/convert_element_type | solution.py:32
  0.7 0.1 stack_broadcast_in_dim.2
  0.7 0.1 multiply_cosine_fusion
  0.9 0.1 pad_maximum_fusion
  1.0 0.6 %select_maximum_fusion.aux_ref = f32[16,8,128]{2,1,0:T(8,128)} fusion(f32[16,1,128]{2,1,0:T(1,128)S(1)} %stack_broadcast_in_dim.2, f32[16,1,128]{2,1,0:T(1,128)S(1)} %bitcast.34, f32[16,1,128]{2,1,0:T(1,128)S(1)} %bitcast.33), kind=kLoop, calls=%fused_computation | loop fusion | flops 98304 | bytes 90112 | tf_op jit(solution)/shard_map/stack | solution.py:664
  1.6 49.8 %decode_step.1 = bf16[16,512]{1,0:T(8,128)(2,1)} custom-call(bf16[16,512]{1,0:T(8,128)(2,1)} %bitcast.35, f32[16,8,128]{2,1,0:T(8,128)} %select_maximum_fusion.aux_ref, f32[1,8192]{1,0:T(1,128)} %bitcast.31, f32[1,8192]{1,0:T(1,128)} %bitcast.32, bf16[8192,512]{1,0:T(8,128)(2,1)} %bitcast.24, bf16[64,8192]{1,0:T(8,128)(2,1)} %bitcast.26, ...), custom_call_target="tpu_custom_call" | custom-call | tf_op jit(solution)/shard_map/decode_step/pallas_call | solution.py:691
  51.4 1.3 %copy.16 = bf16[16,1,512]{2,0,1:T(8,128)(2,1)} copy(bf16[16,1,512]{2,0,1:T(8,128)(2,1)} %bitcast.30) | data formatting | bytes 32768
  (1 shorter events, 0.0 us)
